TPU v7x, 256 devices: a whole 4x4x8 slice. The times are simulated.
256 devices in a mesh: nodes: 64 (over z, x, core), heads: 4 (over y).
Axes of the slice: x: 4, y: 4, z: 8, core: 2. Of those that a mesh axis runs over, the one named last changes fastest.
Arguments:
- nodes_in: bfloat16 [32768, 1024], P('nodes', 'heads'), may hold values from -6 to 6
- local_gain: float32 [1024], replicated, may hold values from 0.5 to 1.5
- neighbour_query_key_value: bfloat16 [3, 1024, 1024], P(None, None, 'heads'), may hold values from -0.25 to 0.25
- local_out: bfloat16 [1024, 1024], P('heads'), may hold values from -0.1875 to 0.1875
- global_gain: float32 [1024], replicated, may hold values from 0.5 to 1.5
- global_qkv: bfloat16 [3, 1024, 1024], P(None, None, 'heads'), may hold values from -0.1875 to 0.1875
- global_out: bfloat16 [1024, 1024], P('heads'), may hold values from -1.875 to 1.875
- feature_map: bfloat16 [16, 64, 128], P('heads'), may hold values from -5 to 5
- neighbour_count: int32 [256], P('nodes'), may hold values from 1 to 8
- neighbour_blocks: int32 [256, 8], P('nodes'), may hold values from 0 to 255, as said below
- metis_order: int32 [256], P('nodes'), may hold values from 0 to 255, as said below
- hashed_order: int32 [256], P('nodes'), may hold values from 0 to 255, as said below
Outputs:
- output: bfloat16 [32768, 1024], P('nodes', 'heads')
Inputs may be any that keep to these rules, and one draw needn't show every extreme that they name: `neighbour_blocks`: entry 0 of block b's list is b itself; every entry lies within 2 blocks of the aligned group of 4 blocks that holds b, inside the graph; entries from neighbour_count on are unused; entries may repeat. `metis_order`: A permutation of the block ids. `hashed_order`: A permutation of the block ids. The blocks at the 4 METIS positions of aligned group g go to the aligned groups of 4 hashed positions numbered (g + k * 16) modulo 64 for k = 0 to 3, exactly 1 of them to each; which block goes to which of these groups, and to which position in it, is drawn.
All inputs are finite; a program needn't handle non-finite values.
Results may differ from a plain program's by a relative error of at most 0.015.
Values may be sent and summed in bfloat16 or wider, within the bound.
No kernel may reach another device: no remote copies, remote signals or barrier semaphores. Data moves between devices by JAX's collectives and lax.ppermute only.
A program may use at most 64 MiB of HBM per device.

v0:
```python
import jax
import jax.numpy as jnp
from jax import lax
from jax.sharding import PartitionSpec as P

HD = 64
BLOCK = 128
HALO_BLK = 2
EPSILON = 1e-06


def passed_along(value, axis, steps):
    count = lax.axis_size(axis)
    pairs = [(source, (source + steps) % count) for source in range(count)]
    return lax.ppermute(value, axis, pairs)


def gathered_total(array, axis):
    parts = lax.all_gather(array, axis)
    return parts.sum(axis=0)


def laid_out(parts, dim):
    parts = jnp.moveaxis(parts, 0, dim)
    dims = parts.shape
    return parts.reshape(*dims[:dim], dims[dim] * dims[dim + 1], *dims[dim + 2 :])


def copy_for_each(array, axis):
    copies = jnp.broadcast_to(array, (lax.axis_size(axis), *array.shape))
    return lax.all_to_all(copies, axis, split_axis=0, concat_axis=0, tiled=True)


def collect(array, axis, dim):
    return laid_out(copy_for_each(array, axis), dim)


def padded(array, sides, width):
    for axis, dim in sides:
        count, length = (lax.axis_size(axis), array.shape[dim])
        up = [(i, (i + 1) % count) for i in range(count - 1)]
        down = [(j, i) for i, j in up]
        last = lax.slice_in_dim(array, length - width, length, axis=dim)
        initial = lax.slice_in_dim(array, 0, width, axis=dim)
        before = lax.ppermute(last, axis, up)
        after = lax.ppermute(initial, axis, down)
        array = jnp.concatenate([before, array, after], axis=dim)
    return array


def cut_along(array, dim, count):
    dims = array.shape
    parts = array.reshape(*dims[:dim], count, dims[dim] // count, *dims[dim + 1 :])
    return jnp.moveaxis(parts, dim, 0)


def summed_on_arrival(array, axis, dim):
    count = lax.axis_size(axis)
    parts = lax.all_to_all(cut_along(array, dim, count), axis, 0, 0, tiled=True)
    return jnp.sum(parts.astype(jnp.float32), axis=0)


def root_scale(row_data, gain_vector):
    as_float = row_data.astype(jnp.float32)
    mean_square = jnp.mean(as_float * as_float, axis=-1, keepdims=True)
    return (as_float * lax.rsqrt(mean_square + EPSILON) * gain_vector).astype(jnp.bfloat16)


def local_attention(queries, extended, counts, local_index):
    block_count = counts.shape[0]
    list_slots = local_index.shape[1]
    group_size = 4
    feature_width = queries.shape[1]
    heads_local = feature_width // HD
    key_blocks = extended.reshape(2, -1, BLOCK, feature_width)
    query_groups = queries.reshape(block_count // group_size, group_size, BLOCK, heads_local, HD)
    slot_of_key = jnp.arange(list_slots * BLOCK, dtype=jnp.int32) // BLOCK

    def one_group(inputs):
        query_group, index_group, count_group = inputs
        picked = key_blocks[:, index_group].reshape(
            2, group_size, list_slots * BLOCK, heads_local, HD
        )
        scores = jnp.einsum(
            "gqhd,gkhd->ghqk", query_group, picked[0], preferred_element_type=jnp.float32
        ) * HD ** (-0.5)
        live = slot_of_key[None, :] < count_group[:, None]
        scores = jnp.where(live[:, None, None, :], scores, -jnp.inf)
        row_max = jnp.max(scores, axis=-1, keepdims=True)
        expo = jnp.exp(scores - row_max)
        totals = jnp.sum(expo, axis=-1)
        local_weights = expo.astype(jnp.bfloat16)
        mixed_heads = jnp.einsum(
            "ghqk,gkhd->gqhd", local_weights, picked[1], preferred_element_type=jnp.float32
        )
        mixed_heads = mixed_heads / jnp.transpose(totals, (0, 2, 1))[..., None]
        return mixed_heads.astype(jnp.bfloat16)

    mixed_all = lax.map(
        one_group,
        (
            query_groups,
            local_index.reshape(block_count // group_size, group_size, list_slots),
            counts.reshape(block_count // group_size, group_size),
        ),
    )
    return mixed_all.reshape(block_count * BLOCK, feature_width)


def relayout(row_data, metis_local, all_hashed, device_nodes):
    block_count = metis_local.shape[0]
    devices = lax.axis_size("nodes")
    lane_count = min(block_count, devices)
    stride = max(1, devices // block_count)
    slot_limit = block_count // lane_count
    feature_width = row_data.shape[1]
    total_blocks = all_hashed.shape[0]
    matches = all_hashed[None, :] == metis_local[:, None]
    target = jnp.sum(
        jnp.where(matches, jnp.arange(total_blocks, dtype=jnp.int32)[None, :], 0), axis=1
    )
    steps_away = (target // block_count - device_nodes) % devices // stride
    order_ids = jnp.arange(block_count, dtype=jnp.int32)
    earlier = (steps_away[None, :] == steps_away[:, None]) & (
        order_ids[None, :] < order_ids[:, None]
    )
    rank_within = jnp.sum(earlier.astype(jnp.int32), axis=1)
    lane_id = rank_within * lane_count + steps_away
    chosen = lane_id[None, :] == order_ids[:, None]
    source = jnp.sum(jnp.where(chosen, order_ids[None, :], 0), axis=1)
    lane_target = jnp.sum(jnp.where(chosen, target[None, :], 0), axis=1)
    blocks = row_data.reshape(block_count, BLOCK, feature_width)
    outgoing = blocks[source].reshape(slot_limit, lane_count, BLOCK, feature_width)
    positions = lane_target.reshape(slot_limit, lane_count)
    block_pieces = [outgoing[:, :1]]
    position_pieces = [positions[:, :1]]
    for lane_step in range(1, lane_count):
        arrived, arrived_at = passed_along(
            (outgoing[:, lane_step : lane_step + 1], positions[:, lane_step : lane_step + 1]),
            "nodes",
            lane_step * stride,
        )
        block_pieces.append(arrived)
        position_pieces.append(arrived_at)
    incoming = jnp.concatenate(block_pieces, axis=1)
    in_position = jnp.concatenate(position_pieces, axis=1)
    local_position = in_position.reshape(block_count) - device_nodes * block_count
    located = local_position[None, :] == order_ids[:, None]
    picked_lane = jnp.sum(jnp.where(located, order_ids[None, :], 0), axis=1)
    return incoming.reshape(block_count, BLOCK, feature_width)[picked_lane].reshape(
        block_count * BLOCK, feature_width
    )


def gather_rows(shard_rows):
    return lax.all_gather(shard_rows, "heads", axis=1, tiled=True)


def global_mixing(full_rows, gain_vector, triple_weight, feature_map, out_weight):
    rescaled_input = root_scale(full_rows, gain_vector)
    triple = jnp.einsum(
        "au,nuz->naz", rescaled_input, triple_weight, preferred_element_type=jnp.float32
    ).astype(jnp.bfloat16)
    row_count = full_rows.shape[0]
    heads_local = feature_map.shape[0]

    def feature_maps(head_rows):
        angles = jnp.einsum(
            "nhd,hdf->nhf",
            head_rows.reshape(row_count, heads_local, HD),
            feature_map,
            preferred_element_type=jnp.float32,
        ) * HD ** (-0.5)
        return (jax.nn.elu(angles) + 1.0).astype(jnp.bfloat16)

    phi_query = feature_maps(triple[0])
    phi_key = feature_maps(triple[1])
    head_values = triple[2].reshape(row_count, heads_local, HD)
    summary = jnp.einsum("nhf,nhd->hfd", phi_key, head_values, preferred_element_type=jnp.float32)
    key_total = jnp.sum(phi_key.astype(jnp.float32), axis=0)
    summary, key_total = (gathered_total(summary, "nodes"), gathered_total(key_total, "nodes"))
    query_float = phi_query.astype(jnp.float32)
    numerator = jnp.einsum("nhf,hfd->nhd", query_float, summary, precision=lax.Precision.HIGHEST)
    denominator = jnp.einsum("nhf,hf->nh", query_float, key_total, precision=lax.Precision.HIGHEST)
    global_mixed = (
        (numerator / denominator[..., None])
        .astype(jnp.bfloat16)
        .reshape(row_count, heads_local * HD)
    )
    return jnp.dot(global_mixed, out_weight, preferred_element_type=jnp.float32)


def body(
    nodes_in,
    local_gain,
    neighbour_query_key_value,
    local_out,
    global_gain,
    global_qkv,
    global_out,
    feature_map,
    neighbour_count,
    neighbour_blocks,
    metis_order,
    hashed_order,
):
    block_count = metis_order.shape[0]
    device_nodes = lax.axis_index("nodes")
    all_hashed = collect(hashed_order, "nodes", 0)
    full_input = collect(nodes_in, "heads", 1)
    local_rescaled = root_scale(full_input, local_gain)
    triple = jnp.einsum(
        "au,nuz->naz", local_rescaled, neighbour_query_key_value, preferred_element_type=jnp.float32
    ).astype(jnp.bfloat16)
    rim_rows = HALO_BLK * BLOCK
    extended = padded(triple[1:], (("nodes", 1),), rim_rows)
    first_block = device_nodes * block_count - HALO_BLK
    local_index = neighbour_blocks - first_block
    local_mixed = local_attention(triple[0], extended, neighbour_count, local_index)
    partial_value = jnp.dot(local_mixed, local_out, preferred_element_type=jnp.float32)
    summed = lax.psum_scatter(
        partial_value.astype(jnp.bfloat16), "heads", scatter_dimension=1, tiled=True
    ).astype(jnp.float32)
    hidden = (nodes_in.astype(jnp.float32) + summed).astype(jnp.bfloat16)
    full_rows = gather_rows(hidden)
    global_partial = global_mixing(full_rows, global_gain, global_qkv, feature_map, global_out)
    global_summed = summed_on_arrival(global_partial.astype(jnp.bfloat16), "heads", 1)
    result = (hidden.astype(jnp.float32) + global_summed).astype(jnp.bfloat16)
    result = relayout(result, metis_order, all_hashed, device_nodes)
    return result


def solution(mesh):
    in_specs = (
        P("nodes", "heads"),
        P(),
        P(None, None, "heads"),
        P("heads", None),
        P(),
        P(None, None, "heads"),
        P("heads", None),
        P("heads", None, None),
        P("nodes"),
        P("nodes", None),
        P("nodes"),
        P("nodes"),
    )
    out_specs = P("nodes", "heads")
    return jax.shard_map(body, mesh=mesh, in_specs=in_specs, out_specs=out_specs, check_vma=False)
```

profile of v0, /device:TPU:33, one launch (start us, length us, event | category | flops | bytes accessed | tf_op | source)
XLA Modules:
  0.0 270.1 jit_solution(14255202605277190932)
XLA Ops:
  6.5 2.2 broadcast_in_dim.96
  8.7 4.2 %all-to-all-start = ((bf16[4,512,256]{2,1,0:T(8,128)(2,1)}), bf16[4,512,256]{2,1,0:T(8,128)(2,1)}, u32[]{:S(2)}, u32[]{:S(2)}) async-start(bf16[4,512,256]{2,1,0:T(8,128)(2,1)} %broadcast_in_dim.96), calls=%async_computation | async-start | bytes 2097152 | tf_op jit(solution)/shard_map/all_to_all | solution.py:31
  13.1 14.1 %all-to-all-done = bf16[4,512,256]{2,1,0:T(8,128)(2,1)} async-done(((bf16[4,512,256]{2,1,0:T(8,128)(2,1)}), bf16[4,512,256]{2,1,0:T(8,128)(2,1)}, u32[]{:S(2)}, u32[]{:S(2)}) %all-to-all-start) | async-done | bytes 1048608 | tf_op jit(solution)/shard_map/all_to_all | solution.py:31
  30.5 3.7 %collective-permute-start.1 = (bf16[2,256,256]{2,1,0:T(8,128)(2,1)S(1)}, bf16[2,256,256]{2,1,0:T(8,128)(2,1)S(1)}, u32[]{:S(2)}, u32[]{:S(2)}) collective-permute-start(bf16[2,256,256]{2,1,0:T(8,128)(2,1)S(1)} %get-tuple-element.34), channel_id=1, source_target_pairs={{4,0},{8,4},{12,8},{16,12},{20,16},{24,20},{28,24},{32,28},{36,32}... | collective-permute-start | bytes 786440 | tf_op jit(solution)/shard_map/ppermute | solution.py:46
  34.2 3.0 %collective-permute-start = (bf16[2,256,256]{2,1,0:T(8,128)(2,1)S(1)}, bf16[2,256,256]{2,1,0:T(8,128)(2,1)}, u32[]{:S(2)}, u32[]{:S(2)}) collective-permute-start(bf16[2,256,256]{2,1,0:T(8,128)(2,1)S(1)} %get-tuple-element.33), channel_id=1, source_target_pairs={{0,4},{4,8},{8,12},{12,16},{16,20},{20,24},{24,28},{28,32},{32,36}... | collective-permute-start | bytes 786440 | tf_op jit(solution)/shard_map/ppermute | solution.py:45
  41.7 2.8 %gather_fusion = bf16[32,2,128,256]{3,2,1,0:T(8,128)(2,1)} fusion(bf16[2,8,128,256]{3,2,1,0:T(8,128)(2,1)S(1)} %bitcast.121, s32[1024]{0:T(1024)S(1)} %pad_clamp_fusion.2), kind=kCustom, calls=%fused_computation | custom fusion | bytes 8388736 | tf_op jit(solution)/shard_map/while/body/eval_jaxpr/gather | solution.py:81
  44.5 7.5 %copy.37 = bf16[4,8,2,128,256]{3,1,4,0,2:T(8,128)(2,1)} copy(bf16[4,8,2,128,256]{4,3,2,1,0:T(8,128)(2,1)} %bitcast.122) | data formatting | bytes 8388608 | tf_op jit(solution)/shard_map/while/body/eval_jaxpr/gather | solution.py:81
  52.0 4.5 %fusion.50 = (bf16[1,4,8,128,256]{3,2,4,1,0:T(8,128)(2,1)}, bf16[1,4,8,128,256]{3,2,4,1,0:T(8,128)(2,1)}) fusion(bf16[2,4,8,128,256]{3,2,4,1,0:T(8,128)(2,1)} %bitcast.123), kind=kLoop, calls=%fused_computation.104 | loop fusion | bytes 8388608 | tf_op jit(solution)/shard_map/while/body/eval_jaxpr/slice | solution.py:85
  56.5 4.2 %squeeze.19 = bf16[4,1024,4,64]{1,3,2,0:T(8,128)(2,1)} reshape(bf16[1,4,8,128,256]{3,2,4,1,0:T(8,128)(2,1)} %get-tuple-element.20) | data formatting | bytes 4194304 | tf_op jit(solution)/shard_map/while/body/eval_jaxpr/squeeze | solution.py:94
  60.7 4.2 %squeeze.21 = bf16[4,1024,4,64]{1,3,2,0:T(8,128)(2,1)} reshape(bf16[1,4,8,128,256]{3,2,4,1,0:T(8,128)(2,1)} %get-tuple-element.19) | data formatting | bytes 4194304 | tf_op jit(solution)/shard_map/while/body/eval_jaxpr/squeeze | solution.py:85
  64.8 2.9 %fusion = (f32[4,4,128]{2,1,0:T(4,128)S(1)}, f32[4,4,128,1024]{3,2,1,0:T(8,128)S(1)}) fusion(pred[4,1024]{1,0:T(4,128)(4,1)S(1)} %broadcast_compare_fusion, bf16[4,1024,4,64]{1,3,2,0:T(8,128)(2,1)} %squeeze.21, bf16[4,128,4,64]{3,2,1,0:T(4,128)(2,1)S(1)} %reshape.297), kind=kOutput, calls=%fused_computation.5 | convolution fusion | flops 274724864 | bytes 10760192 | tf_op jit(solution)/shard_map/while/body/eval_jaxpr/gqhd,gkhd->ghqk/dot_general | solution.py:84
  67.8 2.1 fusion.1
  69.9 2.2 fusion.34
  73.9 27.8 %reduce-scatter.2.cloned.1.call-done = bf16[512,256]{1,0:T(8,128)(2,1)} async-done(((bf16[512,1024]{1,0:T(8,128)(2,1)}), bf16[512,256]{1,0:T(8,128)(2,1)}) %reduce-scatter.2.cloned.1.call-update) | async-done | bytes 262160 | tf_op jit(solution)/shard_map/reduce_scatter | solution.py:221
  101.6 1.7 add_convert_fusion.1
  103.4 28.0 %all-gather.6.cloned.1.call-done = bf16[512,1024]{1,0:T(8,128)(2,1)} async-done(((bf16[512,256]{1,0:T(8,128)(2,1)}), bf16[512,1024]{1,0:T(8,128)(2,1)}) %all-gather.6.cloned.1.call-update) | async-done | bytes 1048592 | tf_op jit(solution)/shard_map/all_gather | solution.py:156
  131.4 1.5 fusion.6
  132.9 2.4 fusion.14
  137.2 20.2 %all_to_all.16 = s32[64,1,4]{2,1,0:T(1,128)S(1)} all-to-all(s32[64,1,4]{2,1,0:T(1,128)S(1)} %broadcast_in_dim.100), channel_id=1, replica_groups=mesh['nodes'=64,'heads'=4] {'nodes'}, dimensions={0} | all-to-all | bytes 2048 | tf_op jit(solution)/shard_map/all_to_all | solution.py:31
  159.4 48.5 %all-gather.2 = f32[64,4,128]{2,1,0:T(4,128)S(1)} all-gather(f32[1,4,128]{2,1,0:T(4,128)S(1)} %bitcast.138), channel_id=3, replica_groups=mesh['nodes'=64,'heads'=4] {'nodes'}, dimensions={0}, use_global_device_ids=true | all-gather | bytes 133120 | tf_op jit(solution)/shard_map/all_gather | solution.py:19
  209.3 13.4 %all-gather.8.cloned.1.call-done = f32[256,128,64]{1,2,0:T(8,128)} async-done(((f32[4,128,64]{1,2,0:T(8,128)}), f32[256,128,64]{1,2,0:T(8,128)}) %all-gather.8.cloned.1.call-update) | async-done | bytes 8388624 | tf_op jit(solution)/shard_map/all_gather | solution.py:19
  222.7 3.9 %reduce_sum.116 = f32[4,128,64]{1,2,0:T(8,128)S(1)} reduce(f32[64,4,128,64]{2,3,1,0:T(8,128)} %bitcast.124, f32[]{:T(128)} %constant.91.clone.1), dimensions={0}, to_apply=%region_5.6 | reduce | flops 2064384 | bytes 8519684 | tf_op jit(solution)/shard_map/reduce_sum | solution.py:20
  229.1 4.2 %all-to-all-start.1 = ((bf16[4,512,256]{2,1,0:T(8,128)(2,1)}), bf16[4,512,256]{2,1,0:T(8,128)(2,1)S(1)}, u32[]{:S(2)}, u32[]{:S(2)}) async-start(bf16[4,512,256]{2,1,0:T(8,128)(2,1)} %bitcast.126), calls=%async_computation.2 | async-start | bytes 2097152 | tf_op jit(solution)/shard_map/all_to_all | solution.py:59
  233.9 1.8 collective-permute-start.7
  235.8 3.3 %collective-permute-start.6 = (s32[1,1]{1,0:T(1,128)}, s32[1,1]{1,0:T(1,128)}, u32[]{:S(2)}, u32[]{:S(2)}) collective-permute-start(s32[1,1]{1,0:T(1,128)} %get-tuple-element.41), channel_id=1, source_target_pairs={{0,128},{4,132},{8,136},{12,140},{16,144},{20,148},{24,152},{28,15... | collective-permute-start | bytes 20 | tf_op jit(solution)/shard_map/ppermute | solution.py:15
  239.1 3.2 %collective-permute-done.6 = s32[1,1]{1,0:T(1,128)} collective-permute-done((s32[1,1]{1,0:T(1,128)}, s32[1,1]{1,0:T(1,128)}, u32[]{:S(2)}, u32[]{:S(2)}) %collective-permute-start.6) | collective-permute-done | bytes 36 | tf_op jit(solution)/shard_map/ppermute | solution.py:15
  242.3 1.7 collective-permute-done.5
  243.9 2.6 add_subtract_fusion
  248.7 1.9 collective-permute-start.4
  250.7 3.3 %collective-permute-start.3 = (bf16[1,1,128,256]{3,2,1,0:T(8,128)(2,1)S(1)}, bf16[1,1,128,256]{3,2,1,0:T(8,128)(2,1)S(1)}, u32[]{:S(2)}, u32[]{:S(2)}) collective-permute-start(bf16[1,1,128,256]{3,2,1,0:T(8,128)(2,1)S(1)} %get-tuple-element.37), channel_id=1, source_target_pairs={{0,128},{4,132},{8,136},{12,140},{16,144},{20,148},{24,152},{28,15... | collective-permute-start | bytes 196616 | tf_op jit(solution)/shard_map/ppermute | solution.py:15
  254.0 4.9 %collective-permute-done.3 = bf16[1,1,128,256]{3,2,1,0:T(8,128)(2,1)S(1)} collective-permute-done((bf16[1,1,128,256]{3,2,1,0:T(8,128)(2,1)S(1)}, bf16[1,1,128,256]{3,2,1,0:T(8,128)(2,1)S(1)}, u32[]{:S(2)}, u32[]{:S(2)}) %collective-permute-start.3) | collective-permute-done | bytes 65568 | tf_op jit(solution)/shard_map/ppermute | solution.py:15
  258.9 3.4 %collective-permute-done.2 = bf16[1,1,128,256]{3,2,1,0:T(8,128)(2,1)S(1)} collective-permute-done((bf16[1,1,128,256]{3,2,1,0:T(8,128)(2,1)S(1)}, bf16[1,1,128,256]{3,2,1,0:T(8,128)(2,1)S(1)}, u32[]{:S(2)}, u32[]{:S(2)}) %collective-permute-start.2) | collective-permute-done | bytes 65568 | tf_op jit(solution)/shard_map/ppermute | solution.py:15
  (90 shorter events, 21.3 us)
Async XLA Ops:
  6.5 22.8 %copy-start = (bf16[3,1024,256]{2,1,0:T(8,128)(2,1)S(1)}, bf16[3,1024,256]{2,1,0:T(8,128)(2,1)}, u32[]{:S(2)}) copy-start(bf16[3,1024,256]{2,1,0:T(8,128)(2,1)} %param.14) | copy-start | bytes 4718596
  6.5 6.5 %copy-start.7 = (s32[4,8]{1,0:T(4,128)S(1)}, s32[4,8]{1,0:T(4,128)}, u32[]{:S(2)}) copy-start(s32[4,8]{1,0:T(4,128)} %param.21) | copy-start | bytes 388
  8.7 18.6 %all-to-all-start = ((bf16[4,512,256]{2,1,0:T(8,128)(2,1)}), bf16[4,512,256]{2,1,0:T(8,128)(2,1)}, u32[]{:S(2)}, u32[]{:S(2)}) async-start(bf16[4,512,256]{2,1,0:T(8,128)(2,1)} %broadcast_in_dim.96), calls=%async_computation | async-start | bytes 2097152 | tf_op jit(solution)/shard_map/all_to_all | solution.py:31
  13.0 16.1 %copy-start.6 = (f32[1024]{0:T(1024)S(1)}, f32[1024]{0:T(1024)}, u32[]{:S(2)}) copy-start(f32[1024]{0:T(1024)} %param.13) | copy-start | bytes 12292
  13.0 88.7 %reduce-scatter.2.cloned.1.call-start = ((), (), s32[]{:S(2)}) async-start(), calls=%async_computation.4 | async-start | bytes 1310720 | tf_op jit(solution)/shard_map/reduce_scatter | solution.py:221
  29.4 7.9 %copy-start.9 = (s32[4]{0:T(128)S(1)}, s32[4]{0:T(128)}, u32[]{:S(2)}) copy-start(s32[4]{0:T(128)} %param.20) | copy-start | bytes 52
  30.5 8.9 %collective-permute-start.1 = (bf16[2,256,256]{2,1,0:T(8,128)(2,1)S(1)}, bf16[2,256,256]{2,1,0:T(8,128)(2,1)S(1)}, u32[]{:S(2)}, u32[]{:S(2)}) collective-permute-start(bf16[2,256,256]{2,1,0:T(8,128)(2,1)S(1)} %get-tuple-element.34), channel_id=1, source_target_pairs={{4,0},{8,4},{12,8},{16,12},{20,16},{24,20},{28,24},{32,28},{36,32}... | collective-permute-start | bytes 786440 | tf_op jit(solution)/shard_map/ppermute | solution.py:46
  34.2 6.3 %collective-permute-start = (bf16[2,256,256]{2,1,0:T(8,128)(2,1)S(1)}, bf16[2,256,256]{2,1,0:T(8,128)(2,1)}, u32[]{:S(2)}, u32[]{:S(2)}) collective-permute-start(bf16[2,256,256]{2,1,0:T(8,128)(2,1)S(1)} %get-tuple-element.33), channel_id=1, source_target_pairs={{0,4},{4,8},{8,12},{12,16},{16,20},{20,24},{24,28},{28,32},{32,36}... | collective-permute-start | bytes 786440 | tf_op jit(solution)/shard_map/ppermute | solution.py:45
  67.8 2.1 copy-start.2
  69.8 2.5 copy-start.4
  72.1 29.6 %copy-start.3 = (bf16[512,256]{1,0:T(8,128)(2,1)S(1)}, bf16[512,256]{1,0:T(8,128)(2,1)}, u32[]{:S(2)}) copy-start(bf16[512,256]{1,0:T(8,128)(2,1)} %param.12) | copy-start | bytes 786436
  72.3 60.6 %copy-start.11 = (bf16[3,1024,256]{2,1,0:T(8,128)(2,1)S(1)}, bf16[3,1024,256]{2,1,0:T(8,128)(2,1)}, u32[]{:S(2)}) copy-start(bf16[3,1024,256]{2,1,0:T(8,128)(2,1)} %param.17) | copy-start | bytes 4718596
  72.3 60.6 %copy-start.13 = (f32[1024]{0:T(1024)S(1)}, f32[1024]{0:T(1024)}, u32[]{:S(2)}) copy-start(f32[1024]{0:T(1024)} %param.16) | copy-start | bytes 12292
  73.8 57.6 %all-gather.6.cloned.1.call-start = ((), (), s32[]{:S(2)}) async-start(), calls=%async_computation.5 | async-start | bytes 1310720 | tf_op jit(solution)/shard_map/all_gather | solution.py:156
  103.4 119.3 %all-gather.8.cloned.1.call-start = ((), (), s32[]{:S(2)}) async-start(), calls=%async_computation.6 | async-start | bytes 8519680 | tf_op jit(solution)/shard_map/all_gather | solution.py:19
  132.9 2.5 copy-start.12
  135.4 1.7 copy-start.8
  135.4 23.4 %copy-start.10 = (s32[4]{0:T(128)S(1)}, s32[4]{0:T(128)}, u32[]{:S(2)}) copy-start(s32[4]{0:T(128)} %param.22) | copy-start | bytes 52
  226.5 1.0 copy-start.5
  229.1 19.0 %copy-start.1 = (bf16[512,256]{1,0:T(8,128)(2,1)S(1)}, bf16[512,256]{1,0:T(8,128)(2,1)}, u32[]{:S(2)}) copy-start(bf16[512,256]{1,0:T(8,128)(2,1)} %add_convert_fusion.1) | copy-start | bytes 786436
  229.1 18.8 %all-to-all-start.1 = ((bf16[4,512,256]{2,1,0:T(8,128)(2,1)}), bf16[4,512,256]{2,1,0:T(8,128)(2,1)S(1)}, u32[]{:S(2)}, u32[]{:S(2)}) async-start(bf16[4,512,256]{2,1,0:T(8,128)(2,1)} %bitcast.126), calls=%async_computation.2 | async-start | bytes 2097152 | tf_op jit(solution)/shard_map/all_to_all | solution.py:59
  233.9 5.2 %collective-permute-start.7 = (s32[1,1]{1,0:T(1,128)}, s32[1,1]{1,0:T(1,128)}, u32[]{:S(2)}, u32[]{:S(2)}) collective-permute-start(s32[1,1]{1,0:T(1,128)} %get-tuple-element.40), channel_id=1, source_target_pairs={{0,192},{4,196},{8,200},{12,204},{16,208},{20,212},{24,216},{28,22... | collective-permute-start | bytes 20 | tf_op jit(solution)/shard_map/ppermute | solution.py:15
  235.8 6.5 %collective-permute-start.6 = (s32[1,1]{1,0:T(1,128)}, s32[1,1]{1,0:T(1,128)}, u32[]{:S(2)}, u32[]{:S(2)}) collective-permute-start(s32[1,1]{1,0:T(1,128)} %get-tuple-element.41), channel_id=1, source_target_pairs={{0,128},{4,132},{8,136},{12,140},{16,144},{20,148},{24,152},{28,15... | collective-permute-start | bytes 20 | tf_op jit(solution)/shard_map/ppermute | solution.py:15
  239.1 4.8 %collective-permute-start.5 = (s32[1,1]{1,0:T(1,128)}, s32[1,1]{1,0:T(1,128)}, u32[]{:S(2)}, u32[]{:S(2)}) collective-permute-start(s32[1,1]{1,0:T(1,128)} %get-tuple-element.42), channel_id=1, source_target_pairs={{0,64},{4,68},{8,72},{12,76},{16,80},{20,84},{24,88},{28,92},{32,9... | collective-permute-start | bytes 20 | tf_op jit(solution)/shard_map/ppermute | solution.py:15
  248.7 5.2 %collective-permute-start.4 = (bf16[1,1,128,256]{3,2,1,0:T(8,128)(2,1)S(1)}, bf16[1,1,128,256]{3,2,1,0:T(8,128)(2,1)S(1)}, u32[]{:S(2)}, u32[]{:S(2)}) collective-permute-start(bf16[1,1,128,256]{3,2,1,0:T(8,128)(2,1)S(1)} %get-tuple-element.36), channel_id=1, source_target_pairs={{0,192},{4,196},{8,200},{12,204},{16,208},{20,212},{24,216},{28,22... | collective-permute-start | bytes 196616 | tf_op jit(solution)/shard_map/ppermute | solution.py:15
  250.7 8.2 %collective-permute-start.3 = (bf16[1,1,128,256]{3,2,1,0:T(8,128)(2,1)S(1)}, bf16[1,1,128,256]{3,2,1,0:T(8,128)(2,1)S(1)}, u32[]{:S(2)}, u32[]{:S(2)}) collective-permute-start(bf16[1,1,128,256]{3,2,1,0:T(8,128)(2,1)S(1)} %get-tuple-element.37), channel_id=1, source_target_pairs={{0,128},{4,132},{8,136},{12,140},{16,144},{20,148},{24,152},{28,15... | collective-permute-start | bytes 196616 | tf_op jit(solution)/shard_map/ppermute | solution.py:15
  254.0 8.3 %collective-permute-start.2 = (bf16[1,1,128,256]{3,2,1,0:T(8,128)(2,1)S(1)}, bf16[1,1,128,256]{3,2,1,0:T(8,128)(2,1)S(1)}, u32[]{:S(2)}, u32[]{:S(2)}) collective-permute-start(bf16[1,1,128,256]{3,2,1,0:T(8,128)(2,1)S(1)} %get-tuple-element.38), channel_id=1, source_target_pairs={{0,64},{4,68},{8,72},{12,76},{16,80},{20,84},{24,88},{28,92},{32,9... | collective-permute-start | bytes 196616 | tf_op jit(solution)/shard_map/ppermute | solution.py:15
Sparse Core Ops, SparseCore 0:
  73.9 27.6 reduce-scatter.1
  103.5 27.8 all-gather.5
  137.2 85.3 all-gather.7
where the time goes:
time: 271 us; the launch traced here: 270 us
  waiting for transfers between devices  99.8 us (37%)
  blocking collectives  68.7 us (25%)
  local copies, waits for them, and re-layouts  33 us (12%)
  starting transfers between devices  25.6 us (9%)
  other arithmetic  15.4 us (6%)
  matrix products  14 us (5%)
  between operations  13.5 us (5%)
    all_gather x1, blocking collectives, gathered_total(): parts = lax.all_gather(array, axis)  48.5 us
    all_gather x1, waiting for transfers between devices, gather_rows(): return lax.all_gather(shard_rows, 'heads', axis=1, tiled=True)  28 us
    reduce_scatter x1, waiting for transfers between devices, body(): lax.psum_scatter(partial_value.astype(jnp.bfloat16), 'heads', scatter_dim...  27.8 us
    all_to_all x1, blocking collectives, copy_for_each(): return lax.all_to_all(copies, axis, split_axis=0, concat_axis=0, tiled=True)  20.2 us
    all_to_all x1, waiting for transfers between devices, copy_for_each(): return lax.all_to_all(copies, axis, split_axis=0, concat_axis=0, tiled=True)  14.1 us
    all_gather x1, waiting for transfers between devices, gathered_total(): parts = lax.all_gather(array, axis)  13.4 us
    ppermute x6, waiting for transfers between devices, passed_along(): return lax.ppermute(value, axis, pairs)  13.1 us
    ppermute x6, starting transfers between devices, passed_along(): return lax.ppermute(value, axis, pairs)  10.4 us
  transfers between devices with their start and end apart: 13, of which 11 were waited for; matrix products, arithmetic and copies ran while one was open for 3% of the time, Pallas kernels for 0%

commit v1 on v0

--- a/solution.py
+++ b/solution.py
@@ -153,7 +153,14 @@
 
 
 def gather_rows(shard_rows):
-    return lax.all_gather(shard_rows, "heads", axis=1, tiled=True)
+
+    def pair_wires(unit, group_axis, axis_k):
+        spare = lax.psum(1, group_axis)
+        known = jnp.stack(spare * [unit])
+        formed = lax.all_to_all(known, group_axis, 0, 0)
+        return jnp.concatenate(formed, axis=axis_k)
+
+    return pair_wires(shard_rows, "heads", 1)
 
 
 def global_mixing(full_rows, gain_vector, triple_weight, feature_map, out_weight):

time: 271 us -> 258 us (0.952)
  waiting for transfers between devices: 99.8 us -> 70.6 us
  blocking collectives: 68.7 us -> 86 us
    all_gather x1 -> x0, waiting for transfers between devices: 28 us -> none  [gather_rows(): return lax.all_gather(shard_rows, 'heads', axis=1, tiled=True)]
    all_to_all x0 -> x1, blocking collectives: none -> 15.8 us  [pair_wires(): formed = lax.all_to_all(known, group_axis, 0, 0)]
  transfers between devices with their start and end apart: 13 -> 12, of which waited for: 11 -> 10; matrix products, arithmetic and copies ran while one was open for 3% -> 3% of each run, Pallas kernels for 0% -> 0%
where the time goes in v1:
time: 258 us; the launch traced here: 257 us
  blocking collectives  86 us (33%)
  waiting for transfers between devices  70.6 us (27%)
  local copies, waits for them, and re-layouts  35.3 us (14%)
  starting transfers between devices  25.5 us (10%)
  between operations  13.8 us (5%)
  other arithmetic  13.7 us (5%)
  matrix products  12.7 us (5%)
    all_gather x1, blocking collectives, gathered_total(): parts = lax.all_gather(array, axis)  48.5 us
    reduce_scatter x1, waiting for transfers between devices, body(): lax.psum_scatter(partial_value.astype(jnp.bfloat16), 'heads', scatter_dim...  27.8 us
    all_to_all x1, blocking collectives, copy_for_each(): return lax.all_to_all(copies, axis, split_axis=0, concat_axis=0, tiled=True)  21.7 us
    all_to_all x1, blocking collectives, pair_wires(): formed = lax.all_to_all(known, group_axis, 0, 0)  15.8 us
    all_to_all x1, waiting for transfers between devices, copy_for_each(): return lax.all_to_all(copies, axis, split_axis=0, concat_axis=0, tiled=True)  14.1 us
    ppermute x6, waiting for transfers between devices, passed_along(): return lax.ppermute(value, axis, pairs)  13.1 us
    all_gather x1, waiting for transfers between devices, gathered_total(): parts = lax.all_gather(array, axis)  12 us
    ppermute x6, starting transfers between devices, passed_along(): return lax.ppermute(value, axis, pairs)  10.4 us
  transfers between devices with their start and end apart: 12, of which 10 were waited for; matrix products, arithmetic and copies ran while one was open for 3% of the time, Pallas kernels for 0%

profile of v1, /device:TPU:33, one launch (start us, length us, event | category | flops | bytes accessed | tf_op | source)
XLA Modules:
  0.0 257.4 jit_solution(4572680112606435435)
XLA Ops:
  6.5 2.2 broadcast_in_dim.96
  8.7 4.2 %all-to-all-start = ((bf16[4,512,256]{2,1,0:T(8,128)(2,1)}), bf16[4,512,256]{2,1,0:T(8,128)(2,1)}, u32[]{:S(2)}, u32[]{:S(2)}) async-start(bf16[4,512,256]{2,1,0:T(8,128)(2,1)} %broadcast_in_dim.96), calls=%async_computation | async-start | bytes 2097152 | tf_op jit(solution)/shard_map/all_to_all | solution.py:31
  13.1 14.1 %all-to-all-done = bf16[4,512,256]{2,1,0:T(8,128)(2,1)} async-done(((bf16[4,512,256]{2,1,0:T(8,128)(2,1)}), bf16[4,512,256]{2,1,0:T(8,128)(2,1)}, u32[]{:S(2)}, u32[]{:S(2)}) %all-to-all-start) | async-done | bytes 1048608 | tf_op jit(solution)/shard_map/all_to_all | solution.py:31
  27.3 1.5 copy.37
  30.5 3.7 %collective-permute-start.1 = (bf16[2,256,256]{2,1,0:T(8,128)(2,1)S(1)}, bf16[2,256,256]{2,1,0:T(8,128)(2,1)S(1)}, u32[]{:S(2)}, u32[]{:S(2)}) collective-permute-start(bf16[2,256,256]{2,1,0:T(8,128)(2,1)S(1)} %get-tuple-element.34), channel_id=1, source_target_pairs={{4,0},{8,4},{12,8},{16,12},{20,16},{24,20},{28,24},{32,28},{36,32}... | collective-permute-start | bytes 786440 | tf_op jit(solution)/shard_map/ppermute | solution.py:46
  34.2 3.0 %collective-permute-start = (bf16[2,256,256]{2,1,0:T(8,128)(2,1)S(1)}, bf16[2,256,256]{2,1,0:T(8,128)(2,1)}, u32[]{:S(2)}, u32[]{:S(2)}) collective-permute-start(bf16[2,256,256]{2,1,0:T(8,128)(2,1)S(1)} %get-tuple-element.33), channel_id=1, source_target_pairs={{0,4},{4,8},{8,12},{12,16},{16,20},{20,24},{24,28},{28,32},{32,36}... | collective-permute-start | bytes 786440 | tf_op jit(solution)/shard_map/ppermute | solution.py:45
  41.7 2.8 %gather_fusion = bf16[32,2,128,256]{3,2,1,0:T(8,128)(2,1)} fusion(bf16[2,8,128,256]{3,2,1,0:T(8,128)(2,1)S(1)} %bitcast.129, s32[1024]{0:T(1024)S(1)} %pad_clamp_fusion.2), kind=kCustom, calls=%fused_computation | custom fusion | bytes 8388736 | tf_op jit(solution)/shard_map/while/body/eval_jaxpr/gather | solution.py:81
  44.5 7.5 %copy.39 = bf16[4,8,2,128,256]{3,1,4,0,2:T(8,128)(2,1)} copy(bf16[4,8,2,128,256]{4,3,2,1,0:T(8,128)(2,1)} %bitcast.130) | data formatting | bytes 8388608 | tf_op jit(solution)/shard_map/while/body/eval_jaxpr/gather | solution.py:81
  52.0 4.5 %fusion.46 = (bf16[1,4,8,128,256]{3,2,4,1,0:T(8,128)(2,1)}, bf16[1,4,8,128,256]{3,2,4,1,0:T(8,128)(2,1)}) fusion(bf16[2,4,8,128,256]{3,2,4,1,0:T(8,128)(2,1)} %bitcast.131), kind=kLoop, calls=%fused_computation.101 | loop fusion | bytes 8388608 | tf_op jit(solution)/shard_map/while/body/eval_jaxpr/slice | solution.py:85
  56.5 4.2 %squeeze.19 = bf16[4,1024,4,64]{1,3,2,0:T(8,128)(2,1)} reshape(bf16[1,4,8,128,256]{3,2,4,1,0:T(8,128)(2,1)} %get-tuple-element.20) | data formatting | bytes 4194304 | tf_op jit(solution)/shard_map/while/body/eval_jaxpr/squeeze | solution.py:94
  60.7 4.2 %squeeze.21 = bf16[4,1024,4,64]{1,3,2,0:T(8,128)(2,1)} reshape(bf16[1,4,8,128,256]{3,2,4,1,0:T(8,128)(2,1)} %get-tuple-element.19) | data formatting | bytes 4194304 | tf_op jit(solution)/shard_map/while/body/eval_jaxpr/squeeze | solution.py:85
  64.8 2.9 %fusion = (f32[4,4,128]{2,1,0:T(4,128)S(1)}, f32[4,4,128,1024]{3,2,1,0:T(8,128)S(1)}) fusion(pred[4,1024]{1,0:T(4,128)(4,1)S(1)} %broadcast_compare_fusion, bf16[4,1024,4,64]{1,3,2,0:T(8,128)(2,1)} %squeeze.21, bf16[4,128,4,64]{3,2,1,0:T(4,128)(2,1)S(1)} %reshape.304), kind=kOutput, calls=%fused_computation.5 | convolution fusion | flops 274724864 | bytes 10760192 | tf_op jit(solution)/shard_map/while/body/eval_jaxpr/gqhd,gkhd->ghqk/dot_general | solution.py:84
  67.8 2.1 fusion.1
  69.9 2.2 fusion.30
  72.3 1.5 convolution_convert_fusion.1
  73.9 27.8 %reduce-scatter.2.cloned.1.call-done = bf16[512,256]{1,0:T(8,128)(2,1)} async-done(((bf16[512,1024]{1,0:T(8,128)(2,1)}), bf16[512,256]{1,0:T(8,128)(2,1)}) %reduce-scatter.2.cloned.1.call-update) | async-done | bytes 262160 | tf_op jit(solution)/shard_map/reduce_scatter | solution.py:228
  102.7 15.8 %all_to_all.21 = bf16[4,512,256]{2,1,0:T(8,128)(2,1)} all-to-all(bf16[4,512,256]{2,1,0:T(8,128)(2,1)S(1)} %stack.2), channel_id=1, replica_groups=mesh['nodes'=64,'heads'=4] {'heads'}, dimensions={0} | all-to-all | bytes 2097152 | tf_op jit(solution)/shard_map/all_to_all | solution.py:160
  118.6 1.5 copy.43
  124.3 21.7 %all_to_all.22 = s32[64,1,4]{2,1,0:T(1,128)S(1)} all-to-all(s32[64,1,4]{2,1,0:T(1,128)S(1)} %broadcast_in_dim.100), channel_id=1, replica_groups=mesh['nodes'=64,'heads'=4] {'nodes'}, dimensions={0} | all-to-all | bytes 2048 | tf_op jit(solution)/shard_map/all_to_all | solution.py:31
  147.8 48.5 %all-gather.2 = f32[64,4,128]{2,1,0:T(4,128)S(1)} all-gather(f32[1,4,128]{2,1,0:T(4,128)S(1)} %bitcast.146), channel_id=3, replica_groups=mesh['nodes'=64,'heads'=4] {'nodes'}, dimensions={0}, use_global_device_ids=true | all-gather | bytes 133120 | tf_op jit(solution)/shard_map/all_gather | solution.py:19
  197.6 12.0 %all-gather.5.cloned.1.call-done = f32[256,128,64]{1,2,0:T(8,128)} async-done(((f32[4,128,64]{1,2,0:T(8,128)}), f32[256,128,64]{1,2,0:T(8,128)}) %all-gather.5.cloned.1.call-update) | async-done | bytes 8388624 | tf_op jit(solution)/shard_map/all_gather | solution.py:19
  209.7 3.9 %reduce_sum.116 = f32[4,128,64]{1,2,0:T(8,128)S(1)} reduce(f32[64,4,128,64]{2,3,1,0:T(8,128)} %bitcast.132, f32[]{:T(128)} %constant.91.clone.1), dimensions={0}, to_apply=%region_5.6 | reduce | flops 2064384 | bytes 8519684 | tf_op jit(solution)/shard_map/reduce_sum | solution.py:20
  216.1 4.0 %all-to-all-start.2 = ((bf16[4,512,256]{2,1,0:T(8,128)(2,1)}), bf16[4,512,256]{2,1,0:T(8,128)(2,1)S(1)}, u32[]{:S(2)}, u32[]{:S(2)}) async-start(bf16[4,512,256]{2,1,0:T(8,128)(2,1)} %bitcast.134), calls=%async_computation.3 | async-start | bytes 2097152 | tf_op jit(solution)/shard_map/all_to_all | solution.py:59
  220.8 1.8 collective-permute-start.7
  222.6 3.3 %collective-permute-start.6 = (s32[1,1]{1,0:T(1,128)}, s32[1,1]{1,0:T(1,128)}, u32[]{:S(2)}, u32[]{:S(2)}) collective-permute-start(s32[1,1]{1,0:T(1,128)} %get-tuple-element.41), channel_id=1, source_target_pairs={{0,128},{4,132},{8,136},{12,140},{16,144},{20,148},{24,152},{28,15... | collective-permute-start | bytes 20 | tf_op jit(solution)/shard_map/ppermute | solution.py:15
  226.0 3.0 %collective-permute-done.6 = s32[1,1]{1,0:T(1,128)} collective-permute-done((s32[1,1]{1,0:T(1,128)}, s32[1,1]{1,0:T(1,128)}, u32[]{:S(2)}, u32[]{:S(2)}) %collective-permute-start.6) | collective-permute-done | bytes 36 | tf_op jit(solution)/shard_map/ppermute | solution.py:15
  229.0 1.7 collective-permute-done.5
  230.6 2.6 %add_subtract_fusion = s32[4]{0:T(128)S(1)} fusion(s32[1]{0:T(128)} %bitcast.36, s32[1]{0:T(128)} %bitcast.35, s32[1]{0:T(128)} %bitcast.34, s32[1]{0:T(128)} %bitcast.33, s32[]{:T(128)S(6)} %mul.74), kind=kLoop, calls=%fused_computation.97 | loop fusion | flops 16 | bytes 36 | tf_op jit(solution)/shard_map/sub | solution.py:147
  235.6 1.9 collective-permute-start.4
  237.5 3.3 %collective-permute-start.3 = (bf16[1,1,128,256]{3,2,1,0:T(8,128)(2,1)S(1)}, bf16[1,1,128,256]{3,2,1,0:T(8,128)(2,1)S(1)}, u32[]{:S(2)}, u32[]{:S(2)}) collective-permute-start(bf16[1,1,128,256]{3,2,1,0:T(8,128)(2,1)S(1)} %get-tuple-element.37), channel_id=1, source_target_pairs={{0,128},{4,132},{8,136},{12,140},{16,144},{20,148},{24,152},{28,15... | collective-permute-start | bytes 196616 | tf_op jit(solution)/shard_map/ppermute | solution.py:15
  240.8 4.8 %collective-permute-done.3 = bf16[1,1,128,256]{3,2,1,0:T(8,128)(2,1)S(1)} collective-permute-done((bf16[1,1,128,256]{3,2,1,0:T(8,128)(2,1)S(1)}, bf16[1,1,128,256]{3,2,1,0:T(8,128)(2,1)S(1)}, u32[]{:S(2)}, u32[]{:S(2)}) %collective-permute-start.3) | collective-permute-done | bytes 65568 | tf_op jit(solution)/shard_map/ppermute | solution.py:15
  245.6 3.7 %collective-permute-done.2 = bf16[1,1,128,256]{3,2,1,0:T(8,128)(2,1)S(1)} collective-permute-done((bf16[1,1,128,256]{3,2,1,0:T(8,128)(2,1)S(1)}, bf16[1,1,128,256]{3,2,1,0:T(8,128)(2,1)S(1)}, u32[]{:S(2)}, u32[]{:S(2)}) %collective-permute-start.2) | collective-permute-done | bytes 65568 | tf_op jit(solution)/shard_map/ppermute | solution.py:15
  (89 shorter events, 21.8 us)
Async XLA Ops:
  6.5 22.8 %copy-start = (bf16[3,1024,256]{2,1,0:T(8,128)(2,1)S(1)}, bf16[3,1024,256]{2,1,0:T(8,128)(2,1)}, u32[]{:S(2)}) copy-start(bf16[3,1024,256]{2,1,0:T(8,128)(2,1)} %param.14) | copy-start | bytes 4718596
  6.5 6.5 %copy-start.7 = (s32[4,8]{1,0:T(4,128)S(1)}, s32[4,8]{1,0:T(4,128)}, u32[]{:S(2)}) copy-start(s32[4,8]{1,0:T(4,128)} %param.21) | copy-start | bytes 388
  8.7 18.6 %all-to-all-start = ((bf16[4,512,256]{2,1,0:T(8,128)(2,1)}), bf16[4,512,256]{2,1,0:T(8,128)(2,1)}, u32[]{:S(2)}, u32[]{:S(2)}) async-start(bf16[4,512,256]{2,1,0:T(8,128)(2,1)} %broadcast_in_dim.96), calls=%async_computation | async-start | bytes 2097152 | tf_op jit(solution)/shard_map/all_to_all | solution.py:31
  13.0 16.1 %copy-start.5 = (f32[1024]{0:T(1024)S(1)}, f32[1024]{0:T(1024)}, u32[]{:S(2)}) copy-start(f32[1024]{0:T(1024)} %param.13) | copy-start | bytes 12292
  13.0 88.6 %reduce-scatter.2.cloned.1.call-start = ((), (), s32[]{:S(2)}) async-start(), calls=%async_computation.5 | async-start | bytes 1310720 | tf_op jit(solution)/shard_map/reduce_scatter | solution.py:228
  29.4 7.9 %copy-start.9 = (s32[4]{0:T(128)S(1)}, s32[4]{0:T(128)}, u32[]{:S(2)}) copy-start(s32[4]{0:T(128)} %param.20) | copy-start | bytes 52
  30.5 8.9 %collective-permute-start.1 = (bf16[2,256,256]{2,1,0:T(8,128)(2,1)S(1)}, bf16[2,256,256]{2,1,0:T(8,128)(2,1)S(1)}, u32[]{:S(2)}, u32[]{:S(2)}) collective-permute-start(bf16[2,256,256]{2,1,0:T(8,128)(2,1)S(1)} %get-tuple-element.34), channel_id=1, source_target_pairs={{4,0},{8,4},{12,8},{16,12},{20,16},{24,20},{28,24},{32,28},{36,32}... | collective-permute-start | bytes 786440 | tf_op jit(solution)/shard_map/ppermute | solution.py:46
  34.2 6.3 %collective-permute-start = (bf16[2,256,256]{2,1,0:T(8,128)(2,1)S(1)}, bf16[2,256,256]{2,1,0:T(8,128)(2,1)}, u32[]{:S(2)}, u32[]{:S(2)}) collective-permute-start(bf16[2,256,256]{2,1,0:T(8,128)(2,1)S(1)} %get-tuple-element.33), channel_id=1, source_target_pairs={{0,4},{4,8},{8,12},{12,16},{16,20},{20,24},{24,28},{28,32},{32,36}... | collective-permute-start | bytes 786440 | tf_op jit(solution)/shard_map/ppermute | solution.py:45
  67.8 2.1 copy-start.1
  69.8 2.5 copy-start.3
  72.1 29.5 %copy-start.2 = (bf16[512,256]{1,0:T(8,128)(2,1)S(1)}, bf16[512,256]{1,0:T(8,128)(2,1)}, u32[]{:S(2)}) copy-start(bf16[512,256]{1,0:T(8,128)(2,1)} %param.12) | copy-start | bytes 786436
  73.8 135.9 %all-gather.5.cloned.1.call-start = ((), (), s32[]{:S(2)}) async-start(), calls=%async_computation.6 | async-start | bytes 8519680 | tf_op jit(solution)/shard_map/all_gather | solution.py:19
  118.6 1.8 copy-start.6
  120.1 1.4 copy-start.11
  121.5 1.1 copy-start.12
  122.6 1.7 copy-start.8
  122.6 24.7 %copy-start.10 = (s32[4]{0:T(128)S(1)}, s32[4]{0:T(128)}, u32[]{:S(2)}) copy-start(s32[4]{0:T(128)} %param.22) | copy-start | bytes 52
  213.5 1.0 copy-start.4
  216.1 18.7 %all-to-all-start.2 = ((bf16[4,512,256]{2,1,0:T(8,128)(2,1)}), bf16[4,512,256]{2,1,0:T(8,128)(2,1)S(1)}, u32[]{:S(2)}, u32[]{:S(2)}) async-start(bf16[4,512,256]{2,1,0:T(8,128)(2,1)} %bitcast.134), calls=%async_computation.3 | async-start | bytes 2097152 | tf_op jit(solution)/shard_map/all_to_all | solution.py:59
  220.8 5.2 %collective-permute-start.7 = (s32[1,1]{1,0:T(1,128)}, s32[1,1]{1,0:T(1,128)}, u32[]{:S(2)}, u32[]{:S(2)}) collective-permute-start(s32[1,1]{1,0:T(1,128)} %get-tuple-element.40), channel_id=1, source_target_pairs={{0,192},{4,196},{8,200},{12,204},{16,208},{20,212},{24,216},{28,22... | collective-permute-start | bytes 20 | tf_op jit(solution)/shard_map/ppermute | solution.py:15
  222.6 6.3 %collective-permute-start.6 = (s32[1,1]{1,0:T(1,128)}, s32[1,1]{1,0:T(1,128)}, u32[]{:S(2)}, u32[]{:S(2)}) collective-permute-start(s32[1,1]{1,0:T(1,128)} %get-tuple-element.41), channel_id=1, source_target_pairs={{0,128},{4,132},{8,136},{12,140},{16,144},{20,148},{24,152},{28,15... | collective-permute-start | bytes 20 | tf_op jit(solution)/shard_map/ppermute | solution.py:15
  226.0 4.7 %collective-permute-start.5 = (s32[1,1]{1,0:T(1,128)}, s32[1,1]{1,0:T(1,128)}, u32[]{:S(2)}, u32[]{:S(2)}) collective-permute-start(s32[1,1]{1,0:T(1,128)} %get-tuple-element.42), channel_id=1, source_target_pairs={{0,64},{4,68},{8,72},{12,76},{16,80},{20,84},{24,88},{28,92},{32,9... | collective-permute-start | bytes 20 | tf_op jit(solution)/shard_map/ppermute | solution.py:15
  235.6 5.2 %collective-permute-start.4 = (bf16[1,1,128,256]{3,2,1,0:T(8,128)(2,1)S(1)}, bf16[1,1,128,256]{3,2,1,0:T(8,128)(2,1)S(1)}, u32[]{:S(2)}, u32[]{:S(2)}) collective-permute-start(bf16[1,1,128,256]{3,2,1,0:T(8,128)(2,1)S(1)} %get-tuple-element.36), channel_id=1, source_target_pairs={{0,192},{4,196},{8,200},{12,204},{16,208},{20,212},{24,216},{28,22... | collective-permute-start | bytes 196616 | tf_op jit(solution)/shard_map/ppermute | solution.py:15
  237.5 8.1 %collective-permute-start.3 = (bf16[1,1,128,256]{3,2,1,0:T(8,128)(2,1)S(1)}, bf16[1,1,128,256]{3,2,1,0:T(8,128)(2,1)S(1)}, u32[]{:S(2)}, u32[]{:S(2)}) collective-permute-start(bf16[1,1,128,256]{3,2,1,0:T(8,128)(2,1)S(1)} %get-tuple-element.37), channel_id=1, source_target_pairs={{0,128},{4,132},{8,136},{12,140},{16,144},{20,148},{24,152},{28,15... | collective-permute-start | bytes 196616 | tf_op jit(solution)/shard_map/ppermute | solution.py:15
  240.8 8.5 %collective-permute-start.2 = (bf16[1,1,128,256]{3,2,1,0:T(8,128)(2,1)S(1)}, bf16[1,1,128,256]{3,2,1,0:T(8,128)(2,1)S(1)}, u32[]{:S(2)}, u32[]{:S(2)}) collective-permute-start(bf16[1,1,128,256]{3,2,1,0:T(8,128)(2,1)S(1)} %get-tuple-element.38), channel_id=1, source_target_pairs={{0,64},{4,68},{8,72},{12,76},{16,80},{20,84},{24,88},{28,92},{32,9... | collective-permute-start | bytes 196616 | tf_op jit(solution)/shard_map/ppermute | solution.py:15
Sparse Core Ops, SparseCore 0:
  73.9 27.6 reduce-scatter.1
  124.4 85.2 all-gather.4
